TPU v7x, 32 devices: a whole 2x2x4 slice. The times are simulated.
32 devices in a mesh: coarse: 4 (over y, x), fine: 4 (over z), group: 2 (over core).
Axes of the slice: x: 2, y: 2, z: 4, core: 2. Of those that a mesh axis runs over, the one named last changes fastest.
Arguments:
- fresh_keys: bfloat16 [16, 8192, 8, 128], P(None, ('coarse', 'fine'), 'group'), may hold values from -6 to 6
- fresh_values: bfloat16 [16, 8192, 8, 128], P(None, ('coarse', 'fine'), 'group'), may hold values from -6 to 6
- turn_angle: float32 [8192, 64], replicated, may hold values from -3.140625 to 3.140625
- key_gain: float32 [128], replicated, may hold values from 0.25 to 1.75
Outputs:
- decode_keys: bfloat16 [16, 8, 128, 8192], P(('coarse', 'fine'), 'group')
- decode_values: bfloat16 [16, 8192, 8, 128], P(('coarse', 'fine'), None, 'group')
- key_scale: float32 [16, 8, 128], P(('coarse', 'fine'), 'group')
All inputs are finite; a program needn't handle non-finite values. Where the computation divides by a largest or mean magnitude, that divisor is 1e-20 or more.
Results may differ from a plain program's by a relative error of at most 0.001.
Values may be sent and summed in bfloat16 or wider, within the bound.
A program may use at most 128 MiB of HBM per device.

v0:
```python
import jax
import jax.numpy as jnp
from jax import lax
from jax.sharding import PartitionSpec as P


def turn_pairs(vectors, angle):
    half = vectors.shape[-1] // 2
    cosine, sine = (jnp.cos(angle)[None, :, None, :], jnp.sin(angle)[None, :, None, :])
    first, second = (vectors[..., :half], vectors[..., half:])
    return jnp.concatenate(
        [first * cosine - second * sine, second * cosine + first * sine], axis=-1
    )


def root_norm(vectors, row_gain):
    return (
        vectors * lax.rsqrt(jnp.mean(vectors * vectors, axis=-1, keepdims=True) + 1e-06) * row_gain
    )


def ready_to_store(plain_keys, angle, key_gain):
    wide_keys = plain_keys.astype(jnp.float32)
    wide_keys = root_norm(wide_keys, key_gain)
    return turn_pairs(wide_keys, angle)


def local(fresh_keys, fresh_values, turn_angle, key_gain):
    moved_keys, decode_values = (
        lax.all_to_all(fresh_keys, ("coarse", "fine"), split_axis=0, concat_axis=1, tiled=True),
        lax.all_to_all(fresh_values, ("coarse", "fine"), split_axis=0, concat_axis=1, tiled=True),
    )
    turned_keys = ready_to_store(moved_keys, turn_angle, key_gain)
    key_scale = jnp.max(jnp.abs(turned_keys), axis=1)
    narrow_keys = (turned_keys / key_scale[:, None]).astype(jnp.bfloat16)
    decode_keys = jnp.transpose(narrow_keys, (0, 2, 3, 1))
    return (decode_keys, decode_values, key_scale)


def solution(mesh):
    in_specs = (
        P(None, ("coarse", "fine"), "group", None),
        P(None, ("coarse", "fine"), "group", None),
        P(),
        P(),
    )
    out_specs = (
        P(("coarse", "fine"), "group", None, None),
        P(("coarse", "fine"), None, "group", None),
        P(("coarse", "fine"), "group", None),
    )
    return jax.shard_map(local, mesh=mesh, in_specs=in_specs, out_specs=out_specs, check_vma=False)
```

profile of v0, /device:TPU:0, one launch (start us, length us, event | category | flops | bytes accessed | tf_op | source)
XLA Modules:
  0.0 407.9 jit_solution(15231398141940105958)
XLA Ops:
  0.6 193.2 %all_to_all.21 = bf16[16,512,4,128]{3,2,1,0:T(4,128)(2,1)} all-to-all(bf16[16,512,4,128]{3,2,1,0:T(4,128)(2,1)} %param.4), channel_id=1, replica_groups=mesh['coarse'=4,'fine'=4,'group'=2] {'coarse','fine'}, dimensions={0} | all-to-all | bytes 16777216 | tf_op jit(solution)/shard_map/all_to_all | solution.py:30
  193.8 4.7 %all-to-all-start.1 = ((bf16[16,512,4,128]{3,2,1,0:T(4,128)(2,1)}), bf16[16,512,4,128]{3,2,1,0:T(4,128)(2,1)}, u32[]{:S(2)}, u32[]{:S(2)}) async-start(bf16[16,512,4,128]{3,2,1,0:T(4,128)(2,1)} %param.5), calls=%async_computation.1 | async-start | bytes 16777216 | tf_op jit(solution)/shard_map/all_to_all | solution.py:31
  198.6 9.4 %fusion.1 = (f32[8192,64]{0,1:T(8,128)S(1)}, f32[8192,64]{0,1:T(8,128)}) fusion(f32[8192,64]{0,1:T(8,128)} %param.6), kind=kLoop, calls=%fused_computation.9 | loop fusion | bytes 6291456 | tf_op jit(solution)/shard_map/cos | solution.py:9
  208.0 15.8 %copy.10 = f32[1,8192,4,128]{1,3,2,0:T(8,128)} copy(bf16[1,8192,4,128]{3,2,1,0:T(4,128)(2,1)} %bitcast.7) | data formatting | bytes 25165824 | tf_op jit(solution)/shard_map/convert_element_type | solution.py:23
  223.8 11.0 %multiply_reduce_fusion = f32[16,512,4]{2,1,0:T(8,128)S(1)} fusion(bf16[16,512,4,128]{3,2,1,0:T(4,128)(2,1)} %all_to_all.21), kind=kLoop, calls=%fused_computation.4 | loop fusion | flops 12550144 | bytes 8519680 | tf_op jit(solution)/shard_map/reduce_sum | solution.py:18
  234.8 0.0 copy-start.3
  234.8 2.8 add_rsqrt_fusion
  237.6 2.8 copy.9
  240.4 0.0 copy-done.3
  240.4 0.0 copy-start.1
  240.5 12.5 %multiply_multiply_fusion = f32[1,8192,4,128]{1,3,2,0:T(8,128)} fusion(f32[1,8192,4,128]{1,3,2,0:T(8,128)} %copy.10, f32[128]{0:T(128)S(1)} %copy-done.3, f32[8192,4]{0,1:T(4,128)S(1)} %copy.9), kind=kLoop, calls=%fused_computation.3 | loop fusion | flops 8388608 | bytes 33686016 | tf_op jit(solution)/shard_map/mul | solution.py:18
  252.9 0.0 copy-done.1
  252.9 9.6 %multiply_subtract_fusion = (f32[1,8192,4,64]{1,3,2,0:T(8,128)S(1)}, f32[1,8192,4,64]{1,3,2,0:T(8,128)}) fusion(f32[1,8192,4,128]{1,3,2,0:T(8,128)} %multiply_multiply_fusion, f32[8192,64]{0,1:T(8,128)S(1)} %copy-done.1, f32[8192,64]{0,1:T(8,128)S(1)} %get-tuple-element.5), kind=kLoop, calls=%fused_computation.6 | loop fusion | flops 12582912 | bytes 37748736 | tf_op jit(solution)/shard_map/sub | solution.py:12
  262.6 0.0 copy-start
  262.6 5.0 %abs_reduce_fusion = f32[4,128]{1,0:T(4,128)S(1)} fusion(f32[1,8192,4,64]{1,3,2,0:T(8,128)} %get-tuple-element.4, f32[1,8192,4,64]{1,3,2,0:T(8,128)S(1)} %get-tuple-element.3), kind=kLoop, calls=%fused_computation.2 | loop fusion | flops 12582400 | bytes 16779264 | tf_op jit(solution)/shard_map/reduce_max | solution.py:34
  267.6 0.9 copy-done
  268.5 0.0 copy-start.2
  268.5 4.2 %fusion = bf16[1,4,128,8192]{3,2,1,0:T(8,128)(2,1)} fusion(f32[4,128]{1,0:T(4,128)S(1)} %abs_reduce_fusion, f32[1,8192,4,64]{1,3,2,0:T(8,128)S(1)} %copy-done, f32[1,8192,4,64]{1,3,2,0:T(8,128)S(1)} %get-tuple-element.3), kind=kLoop, calls=%fused_computation.7 | loop fusion | flops 12582912 | bytes 25167872 | tf_op jit(solution)/shard_map/transpose | solution.py:36
  272.6 0.0 copy-done.2
  272.6 127.2 %all-to-all-done.1 = bf16[16,512,4,128]{3,2,1,0:T(4,128)(2,1)} async-done(((bf16[16,512,4,128]{3,2,1,0:T(4,128)(2,1)}), bf16[16,512,4,128]{3,2,1,0:T(4,128)(2,1)}, u32[]{:S(2)}, u32[]{:S(2)}) %all-to-all-start.1) | async-done | bytes 8388640 | tf_op jit(solution)/shard_map/all_to_all | solution.py:31
  399.8 8.1 %copy.12 = bf16[1,8192,4,128]{3,2,1,0:T(4,128)(2,1)} copy(bf16[1,8192,4,128]{3,2,1,0:T(4,128)(2,1)} %bitcast.3) | data formatting | bytes 16777216
Async XLA Ops:
  193.8 206.0 %all-to-all-start.1 = ((bf16[16,512,4,128]{3,2,1,0:T(4,128)(2,1)}), bf16[16,512,4,128]{3,2,1,0:T(4,128)(2,1)}, u32[]{:S(2)}, u32[]{:S(2)}) async-start(bf16[16,512,4,128]{3,2,1,0:T(4,128)(2,1)} %param.5), calls=%async_computation.1 | async-start | bytes 16777216 | tf_op jit(solution)/shard_map/all_to_all | solution.py:31
  234.8 5.7 %copy-start.3 = (f32[128]{0:T(128)S(1)}, f32[128]{0:T(128)}, u32[]{:S(2)}) copy-start(f32[128]{0:T(128)} %param.7) | copy-start | bytes 1540
  240.4 12.5 %copy-start.1 = (f32[8192,64]{0,1:T(8,128)S(1)}, f32[8192,64]{0,1:T(8,128)}, u32[]{:S(2)}) copy-start(f32[8192,64]{0,1:T(8,128)} %get-tuple-element.6) | copy-start | bytes 6291460
  262.6 5.9 %copy-start = (f32[1,8192,4,64]{1,3,2,0:T(8,128)S(1)}, f32[1,8192,4,64]{1,3,2,0:T(8,128)}, u32[]{:S(2)}) copy-start(f32[1,8192,4,64]{1,3,2,0:T(8,128)} %get-tuple-element.4) | copy-start | bytes 25165828
  268.5 4.2 %copy-start.2 = (f32[4,128]{1,0:T(4,128)}, f32[4,128]{1,0:T(4,128)S(1)}, u32[]{:S(2)}) copy-start(f32[4,128]{1,0:T(4,128)S(1)} %abs_reduce_fusion) | copy-start | bytes 6148
where the time goes:
time: 409 us; the launch traced here: 408 us
  blocking collectives  193 us (47%)
  waiting for transfers between devices  127 us (31%)
  other arithmetic  45.1 us (11%)
  local copies, waits for them, and re-layouts  37 us (9%)
  starting transfers between devices  4.75 us (1%)
    all_to_all x1, blocking collectives, local(): lax.all_to_all(fresh_keys, ('coarse', 'fine'), split_axis=0, concat_axis=...  193 us
    all_to_all x1, waiting for transfers between devices, local(): lax.all_to_all(fresh_values, ('coarse', 'fine'), split_axis=0, concat_axi...  127 us
    convert_element_type x1, local copies, waits for them, and re-layouts, ready_to_store(): wide_keys = plain_keys.astype(jnp.float32)  15.8 us
    mul x1, other arithmetic, root_norm(): vectors * lax.rsqrt(jnp.mean(vectors * vectors, axis=-1, keepdims=True) +...  12.5 us
    reduce_sum x1, other arithmetic, root_norm(): jnp.mean(vectors * vectors, axis=-1, keepdims=True) + 1e-06  11 us
    sub x1, other arithmetic, turn_pairs(): first * cosine - second * sine  9.65 us
    cos x1, local copies, waits for them, and re-layouts, turn_pairs(): jnp.cos(angle)[None, :, None, :]  9.41 us
    unnamed x9, local copies, waits for them, and re-layouts  8.95 us
  transfers between devices with their start and end apart: 1, of which 1 were waited for; matrix products, arithmetic and copies ran while one was open for 18% of the time, Pallas kernels for 0%

commit v1 on v0

v1 whole, which is shorter than its diff:
```python
import functools

import jax
import jax.numpy as jnp
from jax import lax
from jax.experimental import pallas as pl
from jax.experimental.pallas import tpu as pltpu
from jax.sharding import PartitionSpec as P

MESH = pl.DeviceIdType.MESH
LANES = 128


def partner(me, k, n):
    if n & (n - 1) == 0:
        return me ^ k
    return lax.rem(k - me + n, n)


def order(nc, nf):
    steps = [(i, j) for j in range(nf - 1, -1, -1) for i in range(nc)]
    return steps


def kernel(nc, nf, heads, spots, keys, values, angle, gain, keys_out, values_out, scale_out,
           moved, turned, angles, gains, pick, peak, send_sem, key_sem, value_sem, own_sem):
    n = nc * nf
    size = gain.shape[-1]
    half = size // 2
    c, f, g = (lax.axis_index(a) for a in ("coarse", "fine", "group"))
    me = c * nf + f

    def device(i, j):
        return (i, j, g)

    barrier = pltpu.get_barrier_semaphore()
    for k in range(1, n):
        other = lax.rem(me + k, n)
        pl.semaphore_signal(
            barrier, inc=1, device_id=device(other // nf, lax.rem(other, nf)), device_id_type=MESH
        )
    pl.semaphore_wait(barrier, n - 1)

    steps = order(nc, nf)
    sends = []
    for which, (source, target, sem) in enumerate(((keys, moved, key_sem), (values, values_out, value_sem))):
        for step, (i, j) in enumerate(steps):
            if (i, j) == (0, 0):
                continue
            tc, tf = (partner(c, i, nc), partner(f, j, nf))
            copy = pltpu.make_async_remote_copy(
                src_ref=source.at[tc * nf + tf],
                dst_ref=target.at[me],
                send_sem=send_sem.at[which, step],
                recv_sem=sem.at[me],
                device_id=device(tc, tf),
                device_id_type=MESH,
            )
            copy.start()
            sends.append(copy)
    own_keys = pltpu.make_async_copy(keys.at[me], moved.at[me], own_sem.at[0])
    own_values = pltpu.make_async_copy(values.at[me], values_out.at[me], own_sem.at[1])
    own_angles = pltpu.make_async_copy(angle, angles, own_sem.at[2])
    own_keys.start()
    own_angles.start()
    own_values.start()

    chunk = LANES * heads
    row = lax.broadcasted_iota(jnp.int32, (chunk, chunk), 0)
    column = lax.broadcasted_iota(jnp.int32, (chunk, chunk), 1)
    wanted = (column % LANES) * heads + column // LANES
    pick[...] = jnp.where(row == wanted, 1.0, 0.0).astype(jnp.bfloat16)
    gains[...] = jnp.transpose(jnp.broadcast_to(gain[...], (LANES, size)))
    peak[...] = jnp.zeros_like(peak)
    own_keys.wait()
    own_angles.wait()
    own_values.wait()

    def block(source):
        @pl.loop(0, spots // LANES)
        def _(part):
            rows = pl.ds(pl.multiple_of(part * chunk, chunk), chunk)
            spot = pl.ds(pl.multiple_of(source * spots + part * LANES, LANES), LANES)
            flat = lax.dot_general(
                moved[source, rows, :], pick[...], (((0,), (0,)), ((), ())),
                preferred_element_type=jnp.float32,
            )
            turn = angles[:, spot]
            cosine, sine = (jnp.cos(turn), jnp.sin(turn))
            for h in range(heads):
                wide = flat[:, h * LANES:(h + 1) * LANES]
                power = jnp.sum(wide * wide, axis=0, keepdims=True) * (1.0 / size)
                wide = wide * lax.rsqrt(power + 1e-06) * gains[...]
                first, second = (wide[:half], wide[half:])
                low = first * cosine - second * sine
                high = second * cosine + first * sine
                turned[h, pl.ds(0, half), spot] = low
                turned[h, pl.ds(half, half), spot] = high
                peak[h, pl.ds(0, half), :] = jnp.maximum(peak[h, pl.ds(0, half), :], jnp.abs(low))
                peak[h, pl.ds(half, half), :] = jnp.maximum(peak[h, pl.ds(half, half), :], jnp.abs(high))

    block(me)

    def arrived(target, sem, source):
        return pltpu.make_async_copy(target.at[source], target.at[source], sem.at[source])

    @pl.loop(1, n)
    def _(k):
        step = n - k
        source = partner(c, lax.rem(step, nc), nc) * nf + partner(f, step // nc, nf)
        arrived(moved, key_sem, source).wait()
        block(source)

    for h in range(heads):
        scale_out[pl.ds(h, 1), :] = jnp.max(jnp.transpose(peak[h]), axis=0, keepdims=True)
        peak[h] = jnp.broadcast_to(1.0 / jnp.max(peak[h], axis=1, keepdims=True), (size, LANES))

    @pl.loop(0, n * spots // LANES)
    def _(part):
        spot = pl.ds(pl.multiple_of(part * LANES, LANES), LANES)
        for h in range(heads):
            keys_out[h, :, spot] = (turned[h, :, spot] * peak[h]).astype(jnp.bfloat16)

    @pl.loop(1, n)
    def _(k):
        source = lax.rem(me + k, n)
        arrived(values_out, value_sem, source).wait()

    for copy in sends:
        copy.wait_send()


def local(nc, nf, fresh_keys, fresh_values, turn_angle, key_gain):
    n, spots, heads, size = fresh_keys.shape
    length, half = turn_angle.shape
    rows = spots * heads
    anywhere = pl.BlockSpec(memory_space=pl.ANY)
    inside = pl.BlockSpec(memory_space=pltpu.VMEM)
    keys_out, values_out, scale_out = pl.pallas_call(
        functools.partial(kernel, nc, nf, heads, spots),
        out_shape=(
            pltpu.VMEM((heads, size, length), jnp.bfloat16),
            pltpu.VMEM((n, rows, size), jnp.bfloat16),
            jax.ShapeDtypeStruct((heads, size), jnp.float32),
        ),
        in_specs=[anywhere, anywhere, anywhere, inside],
        out_specs=[inside, inside, inside],
        scratch_shapes=[
            pltpu.VMEM((n, rows, size), jnp.bfloat16),
            pltpu.VMEM((heads, size, length), jnp.float32),
            pltpu.VMEM((half, length), jnp.float32),
            pltpu.VMEM((size, LANES), jnp.float32),
            pltpu.VMEM((LANES * heads, LANES * heads), jnp.bfloat16),
            pltpu.VMEM((heads, size, LANES), jnp.float32),
            pltpu.SemaphoreType.DMA((2, n)),
            pltpu.SemaphoreType.DMA((n,)),
            pltpu.SemaphoreType.DMA((n,)),
            pltpu.SemaphoreType.DMA((3,)),
        ],
        compiler_params=pltpu.CompilerParams(
            collective_id=0, has_side_effects=True, vmem_limit_bytes=36 * 2**20
        ),
    )(
        fresh_keys.reshape(n, rows, size),
        fresh_values.reshape(n, rows, size),
        jnp.transpose(turn_angle),
        key_gain.reshape(1, size),
    )
    return (
        keys_out.reshape(1, heads, size, length),
        values_out.reshape(1, length, heads, size),
        scale_out.reshape(1, heads, size),
    )


def solution(mesh):
    in_specs = (
        P(None, ("coarse", "fine"), "group", None),
        P(None, ("coarse", "fine"), "group", None),
        P(),
        P(),
    )
    out_specs = (
        P(("coarse", "fine"), "group", None, None),
        P(("coarse", "fine"), None, "group", None),
        P(("coarse", "fine"), "group", None),
    )
    run = functools.partial(local, mesh.shape["coarse"], mesh.shape["fine"])
    return jax.shard_map(run, mesh=mesh, in_specs=in_specs, out_specs=out_specs, check_vma=False)
```

time: 409 us -> 395 us (0.966)
  Pallas kernels: 0 us -> 386 us
  blocking collectives: 193 us -> 0 us
  waiting for transfers between devices: 127 us -> 0 us
  other arithmetic: 45.1 us -> 0 us
  local copies, waits for them, and re-layouts: 37 us -> 8.02 us
  starting transfers between devices: 4.75 us -> 0 us
    pallas_call x0 -> x1, Pallas kernels: none -> 386 us  [local(): pl.pallas_call(functools.partial(kernel, nc, nf, heads, spots), out_shape...]
    all_to_all x1 -> x0, blocking collectives: 193 us -> none  [local(): lax.all_to_all(fresh_keys, ('coarse', 'fine'), split_axis=0, concat_axis=...]
    all_to_all x1 -> x0, waiting for transfers between devices: 127 us -> none  [local(): lax.all_to_all(fresh_values, ('coarse', 'fine'), split_axis=0, concat_axi...]
    convert_element_type x1 -> x0, local copies, waits for them, and re-layouts: 15.8 us -> none  [ready_to_store(): wide_keys = plain_keys.astype(jnp.float32)]
    mul x1 -> x0, other arithmetic: 12.5 us -> none  [root_norm(): vectors * lax.rsqrt(jnp.mean(vectors * vectors, axis=-1, keepdims=True) +...]
    reduce_sum x1 -> x0, other arithmetic: 11 us -> none  [root_norm(): jnp.mean(vectors * vectors, axis=-1, keepdims=True) + 1e-06]
    sub x1 -> x0, other arithmetic: 9.65 us -> none  [turn_pairs(): first * cosine - second * sine]
    cos x1 -> x0, local copies, waits for them, and re-layouts: 9.41 us -> none  [turn_pairs(): jnp.cos(angle)[None, :, None, :]]
  transfers between devices with their start and end apart: 1 -> 0, of which waited for: 1 -> 0; matrix products, arithmetic and copies ran while one was open for 18% -> 0% of each run, Pallas kernels for 0% -> 0%
where the time goes in v1:
time: 395 us
  Pallas kernels  386 us (98%)
  local copies, waits for them, and re-layouts  8.02 us (2%)
    pallas_call x1, Pallas kernels, local(): pl.pallas_call(functools.partial(kernel, nc, nf, heads, spots), out_shape...  386 us
    unnamed x5, local copies, waits for them, and re-layouts  8.02 us

profile of v1, /device:TPU:0, one launch (start us, length us, event | category | flops | bytes accessed | tf_op | source)
XLA Modules:
  0.0 394.9 jit_solution(13721829958234665829)
XLA Ops:
  0.6 0.0 copy-start
  0.6 0.6 copy-done
  1.3 386.2 %shard_map.67 = (bf16[4,128,8192]{2,1,0:T(8,128)(2,1)S(1)}, bf16[16,2048,128]{2,1,0:T(8,128)(2,1)S(1)}, f32[4,128]{1,0:T(4,128)S(1)}) custom-call(bf16[16,2048,128]{2,1,0:T(8,128)(2,1)} %bitcast.11, bf16[16,2048,128]{2,1,0:T(8,128)(2,1)} %bitcast.12, f32[64,8192]{1,0:T(8,128)} %bitcast.13, f32[1,128]{1,0:T(1,128)S(1)} %bitcast.10), custom_call_target="tpu_custom_call" | custom-call | tf_op jit(solution)/shard_map/pallas_call | solution.py:139
  387.5 3.4 copy.10
  390.9 3.4 copy.11
  394.3 0.6 copy.12
Async XLA Ops:
  0.6 0.7 copy-start

commit v2 on v1

--- a/solution.py
+++ b/solution.py
@@ -9,6 +9,7 @@
 
 MESH = pl.DeviceIdType.MESH
 LANES = 128
+PIECES = 4
 
 
 def partner(me, k, n):
@@ -17,9 +18,18 @@
     return lax.rem(k - me + n, n)
 
 
-def order(nc, nf):
-    steps = [(i, j) for j in range(nf - 1, -1, -1) for i in range(nc)]
-    return steps
+SPREAD = (
+    (0, 3), (1, 0), (2, 0), (0, 2), (3, 0), (1, 3), (2, 1), (0, 1),
+    (1, 2), (2, 3), (3, 1), (2, 2), (1, 1), (3, 3), (3, 2),
+)
+
+
+def plan(nc, nf):
+    every = [(i, j) for i in range(nc) for j in range(nf - 1, -1, -1) if (i, j) != (0, 0)]
+    steps = [step for step in SPREAD if step in every]
+    steps += [step for step in every if step not in SPREAD]
+    later = [steps[-1]] + steps[1:-1] + [steps[0]]
+    return [(which, i, j) for which, some in enumerate((steps, later)) for i, j in some]
 
 
 def kernel(nc, nf, heads, spots, keys, values, angle, gain, keys_out, values_out, scale_out,
@@ -41,23 +51,20 @@
         )
     pl.semaphore_wait(barrier, n - 1)
 
-    steps = order(nc, nf)
     sends = []
-    for which, (source, target, sem) in enumerate(((keys, moved, key_sem), (values, values_out, value_sem))):
-        for step, (i, j) in enumerate(steps):
-            if (i, j) == (0, 0):
-                continue
-            tc, tf = (partner(c, i, nc), partner(f, j, nf))
-            copy = pltpu.make_async_remote_copy(
-                src_ref=source.at[tc * nf + tf],
-                dst_ref=target.at[me],
-                send_sem=send_sem.at[which, step],
-                recv_sem=sem.at[me],
-                device_id=device(tc, tf),
-                device_id_type=MESH,
-            )
-            copy.start()
-            sends.append(copy)
+    for which, i, j in plan(nc, nf):
+        source, target, sem = ((keys, moved, key_sem), (values, values_out, value_sem))[which]
+        tc, tf = (partner(c, i, nc), partner(f, j, nf))
+        copy = pltpu.make_async_remote_copy(
+            src_ref=source.at[tc * nf + tf],
+            dst_ref=target.at[me],
+            send_sem=send_sem.at[which, i * nf + j],
+            recv_sem=sem.at[me],
+            device_id=device(tc, tf),
+            device_id_type=MESH,
+        )
+        copy.start()
+        sends.append(copy)
     own_keys = pltpu.make_async_copy(keys.at[me], moved.at[me], own_sem.at[0])
     own_values = pltpu.make_async_copy(values.at[me], values_out.at[me], own_sem.at[1])
     own_angles = pltpu.make_async_copy(angle, angles, own_sem.at[2])
@@ -130,6 +137,20 @@
         copy.wait_send()
 
 
+def leave(keys, values, scale, keys_out, values_out, scale_out, sem):
+    pairs = [(scale, scale_out)]
+    for source, target in ((values, values_out), (keys, keys_out)):
+        cut = source.shape[0] // PIECES or 1
+        pairs += [
+            (source.at[pl.ds(at, cut)], target.at[pl.ds(at, cut)]) for at in range(0, source.shape[0], cut)
+        ]
+    copies = [pltpu.make_async_copy(a, b, sem.at[at]) for at, (a, b) in enumerate(pairs)]
+    for copy in copies:
+        copy.start()
+    for copy in copies:
+        copy.wait()
+
+
 def local(nc, nf, fresh_keys, fresh_values, turn_angle, key_gain):
     n, spots, heads, size = fresh_keys.shape
     length, half = turn_angle.shape
@@ -141,7 +162,7 @@
         out_shape=(
             pltpu.VMEM((heads, size, length), jnp.bfloat16),
             pltpu.VMEM((n, rows, size), jnp.bfloat16),
-            jax.ShapeDtypeStruct((heads, size), jnp.float32),
+            pltpu.VMEM((heads, size), jnp.float32),
         ),
         in_specs=[anywhere, anywhere, anywhere, inside],
         out_specs=[inside, inside, inside],
@@ -166,6 +187,16 @@
         jnp.transpose(turn_angle),
         key_gain.reshape(1, size),
     )
+    keys_out, values_out, scale_out = pl.pallas_call(
+        leave,
+        out_shape=tuple(
+            jax.ShapeDtypeStruct(a.shape, a.dtype) for a in (keys_out, values_out, scale_out)
+        ),
+        in_specs=[inside, inside, inside],
+        out_specs=[anywhere, anywhere, anywhere],
+        scratch_shapes=[pltpu.SemaphoreType.DMA((2 * n + 1,))],
+        compiler_params=pltpu.CompilerParams(vmem_limit_bytes=2**20),
+    )(keys_out, values_out, scale_out)
     return (
         keys_out.reshape(1, heads, size, length),
         values_out.reshape(1, length, heads, size),

time: 395 us -> 374 us (0.947)
  the two profiles are of different devices: /device:TPU:0 before, /device:TPU:9 now
where the time goes in v2:
time: 374 us
  Pallas kernels  373 us (100%)
    pallas_call x1, Pallas kernels, local(): pl.pallas_call(functools.partial(kernel, nc, nf, heads, spots), out_shape...  366 us

profile of v2, /device:TPU:9, one launch (start us, length us, event | category | flops | bytes accessed | tf_op | source)
XLA Modules:
  0.0 373.8 jit_solution(3918513266412418240)
XLA Ops:
  0.6 0.0 copy-start
  0.6 0.6 copy-done
  1.3 366.4 %shard_map.67 = (bf16[4,128,8192]{2,1,0:T(8,128)(2,1)S(1)}, bf16[16,2048,128]{2,1,0:T(8,128)(2,1)S(1)}, f32[4,128]{1,0:T(4,128)S(1)}) custom-call(bf16[16,2048,128]{2,1,0:T(8,128)(2,1)} %bitcast.8, bf16[16,2048,128]{2,1,0:T(8,128)(2,1)} %bitcast.9, f32[64,8192]{1,0:T(8,128)} %bitcast.10, f32[1,128]{1,0:T(1,128)S(1)} %bitcast.7), custom_call_target="tpu_custom_call" | custom-call | tf_op jit(solution)/shard_map/pallas_call | solution.py:160
  367.7 6.2 %shard_map.68 = (bf16[4,128,8192]{2,1,0:T(8,128)(2,1)}, bf16[16,2048,128]{2,1,0:T(8,128)(2,1)}, f32[4,128]{1,0:T(4,128)}) custom-call(bf16[4,128,8192]{2,1,0:T(8,128)(2,1)S(1)} %get-tuple-element.9.keys, bf16[16,2048,128]{2,1,0:T(8,128)(2,1)S(1)} %get-tuple-element.10.values, f32[4,128]{1,0:T(4,128)S(1)} %get-tuple-element.11.scale), custom_call_target="tpu_custom_call" | custom-call | tf_op jit(solution)/shard_map/pallas_call | solution.py:190
Async XLA Ops:
  0.6 0.7 copy-start
